TPU v7x, 64 devices: a 2x2x8 block of a 4x4x8 slice. The times are simulated.
64 devices in a mesh: dp: 4 (over x, y), tp: 16 (over z, core).
Axes of the slice: x: 2, y: 2, z: 8, core: 2. Of those that a mesh axis runs over, the one named last changes fastest.
The devices are a block of a 4x4x8 slice.
Arguments:
- enc_out: bfloat16 [4, 2048, 4096], P('dp', 'tp'), parts along dimension 0
- norm_scale: bfloat16 [4096], replicated
- w_key: bfloat16 [6, 4096, 16, 256], P(None, None, 'tp')
- w_value: bfloat16 [6, 4096, 16, 256], P(None, None, 'tp')
Outputs:
- output 1: bfloat16 [6, 4, 2048, 16, 256], P(None, 'dp', None, 'tp'), parts along dimension 1
- output 2: bfloat16 [6, 4, 2048, 16, 256], P(None, 'dp', None, 'tp'), parts along dimension 1
There are 4 independent parts. A program takes and returns all parts, laid end to end along the dimension named above; an argument that names none is the same for every part.
All inputs are finite; a program needn't handle non-finite values.
Results may differ from a plain program's by a relative error of at most 0.001.
Values are sent between devices in bfloat16 or wider.
A program may use at most 768 MiB of HBM per device.

v0:
```python
import jax
import jax.numpy as jnp
from jax import lax
from jax.sharding import PartitionSpec as P

NORM_EPS = 1e-6


def rms_norm(enc_out, norm_scale):
    acts = enc_out.astype(jnp.float32)
    mean_sq = jnp.mean(acts * acts, axis=-1, keepdims=True)
    return (acts * lax.rsqrt(mean_sq + NORM_EPS) * norm_scale.astype(jnp.float32)).astype(jnp.bfloat16)


def solution(mesh):
    def per_device(enc_out, norm_scale, w_key, w_value):
        normed = rms_norm(enc_out, norm_scale)
        gathered = lax.all_gather(normed, "tp", axis=1, tiled=True)
        key_cache = jnp.einsum("bsd,ldhk->lbshk", gathered, w_key, preferred_element_type=jnp.float32).astype(jnp.bfloat16)
        value_cache = jnp.einsum("bsd,ldhk->lbshk", gathered, w_value, preferred_element_type=jnp.float32).astype(jnp.bfloat16)
        return key_cache, value_cache

    weight_spec = P(None, None, "tp", None)
    cache_spec = P(None, "dp", None, "tp", None)
    return jax.shard_map(per_device, mesh=mesh, in_specs=(P("dp", "tp", None), P(None), weight_spec, weight_spec), out_specs=(cache_spec, cache_spec), check_vma=False)
```

profile of v0, /device:TPU:21, one launch (start us, length us, event | category | flops | bytes accessed | tf_op | source)
XLA Modules:
  0.0 180.1 jit_solution(13862311712914340801)
XLA Ops:
  7.2 0.1 all-gather.2.cloned.1.call-start
  7.2 1.5 fusion.14
  8.8 0.7 convert_element_type.34
  9.5 2.5 %fusion.16 = bf16[1,128,4096]{2,1,0:T(8,128)(2,1)} fusion(bf16[1,128,4096]{2,1,0:T(8,128)(2,1)} %param.4, f32[4096]{0:T(1024)S(1)} %convert_element_type.34, f32[128]{0:T(128)S(1)} %add_rsqrt_fusion), kind=kLoop, calls=%fused_computation.12 | loop fusion | flops 2097152 | bytes 2114048 | tf_op jit(solution)/shard_map/convert_element_type | solution.py:12
  12.0 0.1 all-gather.2.cloned.1.call-update
  12.1 97.2 %all-gather.2.cloned.1.call-done = bf16[1,2048,4096]{2,1,0:T(8,128)(2,1)} async-done(((bf16[1,128,4096]{2,1,0:T(8,128)(2,1)}), bf16[1,2048,4096]{2,1,0:T(8,128)(2,1)}) %all-gather.2.cloned.1.call-update) | async-done | bytes 16777232 | tf_op jit(solution)/shard_map/all_gather | solution.py:18
  109.2 0.0 copy-start
  109.2 33.8 %convert_bitcast_fusion = bf16[6,1,2048,1,256]{4,2,3,1,0:T(8,128)(2,1)} fusion(bf16[6,4096,1,256]{3,1,2,0:T(8,128)(2,1)} %param.7, bf16[1,2048,4096]{2,1,0:T(8,128)(2,1)} %all-gather.2.cloned.1.call-done), kind=kOutput, calls=%fused_computation.6 | convolution fusion | flops 25772949504 | bytes 35651584 | tf_op jit(solution)/shard_map/bsd,ldhk->lbshk/dot_general | solution.py:20
  143.0 0.0 copy-done
  143.0 30.2 %convert_bitcast_fusion.1 = bf16[6,1,2048,1,256]{4,2,3,1,0:T(8,128)(2,1)} fusion(bf16[6,4096,1,256]{3,1,2,0:T(8,128)(2,1)} %param.6, bf16[1,2048,4096]{2,1,0:T(8,128)(2,1)S(1)} %copy-done), kind=kOutput, calls=%fused_computation.7 | convolution fusion | flops 25772949504 | bytes 35651584 | tf_op jit(solution)/shard_map/bsd,ldhk->lbshk/dot_general | solution.py:19
  (1 shorter events, 0.0 us)
Async XLA Ops:
  7.2 102.1 %all-gather.2.cloned.1.call-start = ((), (), s32[]{:S(2)}) async-start(), calls=%async_computation | async-start | bytes 17825792 | tf_op jit(solution)/shard_map/all_gather | solution.py:18
  109.2 33.8 %copy-start = (bf16[1,2048,4096]{2,1,0:T(8,128)(2,1)S(1)}, bf16[1,2048,4096]{2,1,0:T(8,128)(2,1)}, u32[]{:S(2)}) copy-start(bf16[1,2048,4096]{2,1,0:T(8,128)(2,1)} %all-gather.2.cloned.1.call-done) | copy-start | bytes 50331652
Sparse Core Ops, SparseCore 0:
  12.2 97.0 all-gather.1
where the time goes:
time: 180 us
  waiting for transfers between devices  97.2 us (54%)
  matrix products  64 us (36%)
  between operations  14.1 us (8%)
  other arithmetic  4.75 us (3%)
    all_gather x1, waiting for transfers between devices, per_device(): gathered = lax.all_gather(normed, 'tp', axis=1, tiled=True)  97.2 us
    dot_general x1, matrix products, per_device(): jnp.einsum('bsd,ldhk->lbshk', gathered, w_value, preferred_element_type=j...  33.8 us
    dot_general x1, matrix products, per_device(): jnp.einsum('bsd,ldhk->lbshk', gathered, w_key, preferred_element_type=jnp...  30.2 us
  transfers between devices with their start and end apart: 1, of which 1 were waited for; matrix products, arithmetic and copies ran while one was open for 0% of the time, Pallas kernels for 0%

commit v1 on v0

v1 whole, which is shorter than its diff:
```python
import functools

import jax
import jax.numpy as jnp
from jax import lax
from jax.experimental import pallas as pl
from jax.experimental.pallas import tpu as pltpu
from jax.sharding import PartitionSpec as P

NORM_EPS = 1e-6
MESH = pl.DeviceIdType.MESH
NORM_ROWS = 32


def ring_body(n, x_hbm, scale_ref, wk_hbm, wv_hbm, out, acts, tokens, weights, in_sem, w_sem, cw_send, cw_recv, ccw_send, ccw_recv, mate_send, mate_recv):
    me = lax.axis_index("tp")
    mate = me + 1 - 2 * lax.rem(me, 2)
    after = lax.rem(me + 2, n)
    before = lax.rem(me + n - 2, n)
    block, d_model = acts.shape
    half = block // 2
    n_layers, _, both = weights.shape
    head_dim = both // 2
    hops = n // 2 - 1

    x_copy = pltpu.make_async_copy(x_hbm, acts, in_sem)
    x_copy.start()
    w_copies = []
    for layer in range(n_layers):
        w_copies.append((
            pltpu.make_async_copy(wk_hbm.at[layer], weights.at[layer, :, pl.ds(0, head_dim)], w_sem.at[2 * layer]),
            pltpu.make_async_copy(wv_hbm.at[layer], weights.at[layer, :, pl.ds(head_dim, head_dim)], w_sem.at[2 * layer + 1]),
        ))

    barrier = pltpu.get_barrier_semaphore()
    for other in (after, before, mate):
        pl.semaphore_signal(barrier, inc=1, device_id={"tp": other}, device_id_type=MESH)

    scale = scale_ref[...].astype(jnp.float32)
    x_copy.wait()
    for pair in w_copies:
        for copy in pair:
            copy.start()

    def normalize(start):
        @pl.loop(0, half // NORM_ROWS)
        def _(i):
            rows = pl.ds(pl.multiple_of(start + i * NORM_ROWS, NORM_ROWS), NORM_ROWS)
            x = acts[rows, :].astype(jnp.float32)
            mean_sq = jnp.mean(x * x, axis=-1, keepdims=True)
            tokens[0, rows, :] = (x * lax.rsqrt(mean_sq + NORM_EPS) * scale).astype(jnp.bfloat16)

    normalize(0)
    normalize(half)
    pl.semaphore_wait(barrier, 3)

    sends = []

    def send(src, dst, send_sem, recv_sem, other):
        copy = pltpu.make_async_remote_copy(src_ref=src, dst_ref=dst, send_sem=send_sem, recv_sem=recv_sem, device_id={"tp": other}, device_id_type=MESH)
        copy.start()
        sends.append(copy)
        return copy

    def send_ring(slot, forward):
        if forward:
            src = tokens.at[0, pl.ds(half * slot, half)] if slot < 2 else tokens.at[slot - 1, pl.ds(0, half)]
            return send(src, tokens.at[slot + 1, pl.ds(0, half)], cw_send.at[slot], cw_recv.at[slot], after)
        src = tokens.at[0, pl.ds(half * (1 - slot), half)] if slot < 2 else tokens.at[slot - 1, pl.ds(half, half)]
        return send(src, tokens.at[slot + 1, pl.ds(half, half)], ccw_send.at[slot], ccw_recv.at[slot], before)

    def send_mate(step):
        return send(tokens.at[step, pl.ds(0, block)], tokens.at[step, pl.ds(block, block)], mate_send.at[step], mate_recv.at[step], mate)

    def project(step, first):
        @pl.loop(0, n_layers)
        def _(layer):
            if first:
                for side in range(2):
                    pltpu.make_async_copy(wk_hbm.at[layer], weights.at[layer, :, pl.ds(side * head_dim, head_dim)], w_sem.at[2 * layer + side]).wait()
            out[step, layer] = jnp.dot(tokens[step], weights[layer], preferred_element_type=jnp.float32).astype(jnp.bfloat16)

    ring = {}
    for slot in range(2):
        ring[slot] = (send_ring(slot, True), send_ring(slot, False))
    swap = send_mate(0)
    swap.wait_recv()
    project(0, True)
    for slot in range(hops):
        for copy in ring[slot]:
            copy.wait_recv()
        if slot + 2 < hops:
            ring[slot + 2] = (send_ring(slot + 2, True), send_ring(slot + 2, False))
        swap = send_mate(slot + 1)
        swap.wait_recv()
        project(slot + 1, False)
    for copy in sends:
        copy.wait_send()


def place_body(n, block, res, k_hbm, v_hbm, sem):
    me = lax.axis_index("tp")
    mate = me + 1 - 2 * lax.rem(me, 2)
    half = block // 2
    steps, _, _, both = res.shape
    head_dim = both // 2
    copies = []
    for step in range(steps):
        for group in range(4):
            who = me if group < 2 else mate
            if step == 0:
                start = who * block + (group % 2) * half
            else:
                slot = step - 1
                away = 2 + 2 * (slot // 2)
                if group % 2 == 0:
                    start = lax.rem(who + n - away, n) * block + (slot % 2) * half
                else:
                    start = lax.rem(who + away, n) * block + ((slot + 1) % 2) * half
            rows = pl.ds(pl.multiple_of(start, half), half)
            for side, dst in enumerate((k_hbm, v_hbm)):
                copy = pltpu.make_async_copy(res.at[step, :, pl.ds(group * half, half), pl.ds(side * head_dim, head_dim)], dst.at[:, rows, :], sem.at[len(copies)])
                copy.start()
                copies.append(copy)
    for copy in copies:
        copy.wait()


def solution(mesh):
    n = mesh.shape["tp"]

    def per_device(enc_out, norm_scale, w_key, w_value):
        _, block, d_model = enc_out.shape
        n_layers, _, _, head_dim = w_key.shape
        hops = n // 2 - 1
        anywhere = pl.BlockSpec(memory_space=pl.ANY)
        in_vmem = pl.BlockSpec(memory_space=pltpu.VMEM)
        res = pl.pallas_call(
            functools.partial(ring_body, n),
            out_shape=pltpu.VMEM((hops + 1, n_layers, 2 * block, 2 * head_dim), jnp.bfloat16),
            in_specs=[anywhere, in_vmem, anywhere, anywhere],
            out_specs=in_vmem,
            scratch_shapes=[
                pltpu.VMEM((block, d_model), jnp.bfloat16),
                pltpu.VMEM((hops + 1, 2 * block, d_model), jnp.bfloat16),
                pltpu.VMEM((n_layers, d_model, 2 * head_dim), jnp.bfloat16),
                pltpu.SemaphoreType.DMA,
                pltpu.SemaphoreType.DMA((2 * n_layers,)),
                pltpu.SemaphoreType.DMA((hops,)),
                pltpu.SemaphoreType.DMA((hops,)),
                pltpu.SemaphoreType.DMA((hops,)),
                pltpu.SemaphoreType.DMA((hops,)),
                pltpu.SemaphoreType.DMA((hops + 1,)),
                pltpu.SemaphoreType.DMA((hops + 1,)),
            ],
            compiler_params=pltpu.CompilerParams(collective_id=0, has_side_effects=True, vmem_limit_bytes=48 * 1024 * 1024),
            name="ring_project",
        )(enc_out.reshape(block, d_model), norm_scale.reshape(1, d_model), w_key.reshape(n_layers, d_model, head_dim), w_value.reshape(n_layers, d_model, head_dim))
        side = jax.ShapeDtypeStruct((n_layers, n * block, head_dim), jnp.bfloat16)
        keys, values = pl.pallas_call(
            functools.partial(place_body, n, block),
            out_shape=(side, side),
            in_specs=[in_vmem],
            out_specs=(anywhere, anywhere),
            scratch_shapes=[pltpu.SemaphoreType.DMA((8 * (hops + 1),))],
            compiler_params=pltpu.CompilerParams(vmem_limit_bytes=4 * 1024 * 1024),
            name="place",
        )(res)
        shape = (n_layers, 1, n * block, 1, head_dim)
        return keys.reshape(shape), values.reshape(shape)

    weight_spec = P(None, None, "tp", None)
    cache_spec = P(None, "dp", None, "tp", None)
    return jax.shard_map(per_device, mesh=mesh, in_specs=(P("dp", "tp", None), P(None), weight_spec, weight_spec), out_specs=(cache_spec, cache_spec), check_vma=False)
```

time: 180 us -> 108 us (0.60)
  Pallas kernels: 0 us -> 106 us
  waiting for transfers between devices: 97.2 us -> 0 us
  matrix products: 64 us -> 0 us
  between operations: 14.1 us -> 0.64 us
  other arithmetic: 4.75 us -> 0 us
    pallas_call x0 -> x2, Pallas kernels: none -> 106 us  [the longest x1 101 us: per_device(): pl.pallas_call(functools.partial(ring_body, n), out_shape=pltpu.VMEM((hop...]
    all_gather x1 -> x0, waiting for transfers between devices: 97.2 us -> none  [per_device(): gathered = lax.all_gather(normed, 'tp', axis=1, tiled=True)]
    dot_general x2 -> x0, matrix products: 64 us -> none  [the longest x1 33.8 us: per_device(): jnp.einsum('bsd,ldhk->lbshk', gathered, w_value, preferred_element_type=j...]
    convert_element_type x2 -> x0, other arithmetic: 3.22 us -> none  [the longest x1 2.52 us: rms_norm(): (acts * lax.rsqrt(mean_sq + NORM_EPS) * norm_scale.astype(jnp.float32)).a...]
  transfers between devices with their start and end apart: 1 -> 0, of which waited for: 1 -> 0; matrix products, arithmetic and copies ran while one was open for 0% -> 0% of each run, Pallas kernels for 0% -> 0%
where the time goes in v1:
time: 108 us
  Pallas kernels  106 us (98%)
  local copies, waits for them, and re-layouts  1.31 us (1%)
    pallas_call x1, Pallas kernels, per_device(): pl.pallas_call(functools.partial(ring_body, n), out_shape=pltpu.VMEM((hop...  101 us
    pallas_call x1, Pallas kernels, per_device(): pl.pallas_call(functools.partial(place_body, n, block), out_shape=(side,...  5.09 us

profile of v1, /device:TPU:21, one launch (start us, length us, event | category | flops | bytes accessed | tf_op | source)
XLA Modules:
  0.0 108.0 jit_solution(16300950188932463231)
XLA Ops:
  0.6 1.3 %reshape.23.scale_ref = bf16[1,4096]{1,0:T(2,128)(2,1)} reshape(bf16[4096]{0:T(1024)(128)(2,1)} %param.5) | data formatting | bytes 16384 | tf_op jit(solution)/shard_map/reshape | solution.py:158
  1.9 100.9 %ring_project.1.res = bf16[8,6,256,512]{3,2,1,0:T(8,128)(2,1)S(1)} custom-call(bf16[128,4096]{1,0:T(8,128)(2,1)} %bitcast.11, bf16[1,4096]{1,0:T(2,128)(2,1)} %reshape.23.scale_ref, bf16[6,4096,256]{2,1,0:T(8,128)(2,1)} %bitcast.9, bf16[6,4096,256]{2,1,0:T(8,128)(2,1)} %bitcast.10), custom_call_target="tpu_custom_call" | custom-call | tf_op jit(solution)/shard_map/ring_project/pallas_call | solution.py:138
  102.9 5.1 %place.1 = (bf16[6,2048,256]{2,1,0:T(8,128)(2,1)}, bf16[6,2048,256]{2,1,0:T(8,128)(2,1)}) custom-call(bf16[8,6,256,512]{3,2,1,0:T(8,128)(2,1)S(1)} %ring_project.1.res), custom_call_target="tpu_custom_call" | custom-call | tf_op jit(solution)/shard_map/place/pallas_call | solution.py:160

commit v2 on v0

v2 whole, which is shorter than its diff:
```python
import functools

import jax
import jax.numpy as jnp
from jax import lax
from jax.experimental import pallas as pl
from jax.experimental.pallas import tpu as pltpu
from jax.sharding import PartitionSpec as P

NORM_EPS = 1e-6
MESH = pl.DeviceIdType.MESH
NORM_ROWS = 16
PIECES = 4


def ring_body(n, x_hbm, scale_ref, wk_hbm, wv_hbm, out, last, weights, acts, tokens, in_sem, w_sem, cw_send, cw_recv, ccw_send, ccw_recv, mate_send, mate_recv):
    me = lax.axis_index("tp")
    mate = me + 1 - 2 * lax.rem(me, 2)
    after = lax.rem(me + 2, n)
    before = lax.rem(me + n - 2, n)
    block, d_model = acts.shape
    piece = block // PIECES
    n_layers, _, both = weights.shape
    head_dim = both // 2
    arrivals = (n // 2 - 1) * PIECES // 2

    x_copies = []
    for part in (0, 2, 1, 3):
        rows = pl.ds(part * piece, piece)
        x_copies.append(pltpu.make_async_copy(x_hbm.at[rows], acts.at[rows], in_sem.at[part]))
        x_copies[-1].start()
    barrier = pltpu.get_barrier_semaphore()
    for other in (after, before, mate):
        pl.semaphore_signal(barrier, inc=1, device_id={"tp": other}, device_id_type=MESH)
    scale = scale_ref[...].reshape(1, d_model).astype(jnp.float32)

    def load_weights(layer):
        for side, src in enumerate((wk_hbm, wv_hbm)):
            yield pltpu.make_async_copy(src.at[layer], weights.at[layer, :, pl.ds(side * head_dim, head_dim)], w_sem.at[2 * layer + side])

    def normalize(part):
        @pl.loop(0, piece // NORM_ROWS)
        def _(i):
            rows = pl.ds(pl.multiple_of(part * piece + i * NORM_ROWS, NORM_ROWS), NORM_ROWS)
            x = acts[rows, :].astype(jnp.float32)
            mean_sq = jnp.mean(x * x, axis=-1, keepdims=True)
            tokens[0, rows, :] = (x * lax.rsqrt(mean_sq + NORM_EPS) * scale).astype(jnp.bfloat16)

    sends = []
    waits = {}

    def send(name, src, dst, send_sem, recv_sem, other):
        copy = pltpu.make_async_remote_copy(src_ref=src, dst_ref=dst, send_sem=send_sem, recv_sem=recv_sem, device_id={"tp": other}, device_id_type=MESH)
        copy.start()
        sends.append(copy)
        waits[name] = copy

    def landing(j):
        return last if j == arrivals - 1 else tokens.at[j + 2]

    def send_ring(j):
        for side, (send_sem, recv_sem, other) in enumerate(((cw_send, cw_recv, after), (ccw_send, ccw_recv, before))):
            if j < PIECES:
                own = (j + side * PIECES // 2) % PIECES
                src = tokens.at[0, pl.ds(own * piece, piece)]
            else:
                src = landing(j - PIECES).at[pl.ds(side * piece, piece)]
            send((side, j), src, landing(j).at[pl.ds(side * piece, piece)], send_sem.at[j], recv_sem.at[j], other)

    def handle(j):
        waits[0, j].wait_recv()
        waits[1, j].wait_recv()
        if j + PIECES < arrivals:
            send_ring(j + PIECES)
        here = landing(j)
        send((2, j), here.at[pl.ds(0, block // 2)], here.at[pl.ds(block // 2, block // 2)], mate_send.at[j + 1], mate_recv.at[j + 1], mate)

    def swapped(j):
        waits[2, j].wait_recv()

    def project(step, count, layer):
        rows = tokens[pl.ds(step, count)].reshape(count * block, d_model)
        both_sides = jnp.dot(rows, weights[layer], preferred_element_type=jnp.float32).astype(jnp.bfloat16)
        for i in range(count):
            out[step + i, layer] = both_sides[i * block : (i + 1) * block]

    x_copies[0].wait()
    x_copies[1].wait()
    for layer in range(n_layers):
        for copy in load_weights(layer):
            copy.start()
    normalize(0)
    normalize(2)
    pl.semaphore_wait(barrier, 3)
    send_ring(0)
    x_copies[2].wait()
    x_copies[3].wait()
    normalize(1)
    normalize(3)
    for j in range(1, PIECES):
        send_ring(j)
    send((2, -1), tokens.at[0], tokens.at[1], mate_send.at[0], mate_recv.at[0], mate)
    swapped(-1)

    @pl.loop(0, n_layers)
    def _(layer):
        for copy in load_weights(layer):
            copy.wait()
        project(0, 2, layer)

    late = arrivals - 6
    for j in range(0, late, 2):
        handle(j)
        handle(j + 1)
        swapped(j)
        swapped(j + 1)

        @pl.loop(0, n_layers)
        def _(layer):
            project(j + 2, 2, layer)

    handle(late)
    handle(late + 1)
    swapped(late)
    swapped(late + 1)
    for layer in range(n_layers):
        project(late + 2, 2, layer)
        if layer == n_layers // 2:
            handle(late + 2)
    swapped(late + 2)
    for layer in range(n_layers):
        project(late + 4, 1, layer)
        if layer == n_layers - 2:
            handle(late + 3)
    swapped(late + 3)
    for layer in range(n_layers):
        project(late + 5, 1, layer)
    handle(late + 4)
    swapped(late + 4)
    for layer in range(n_layers):
        project(late + 6, 1, layer)
    handle(late + 5)
    swapped(late + 5)
    for copy in sends:
        copy.wait_send()


def place_body(n, res, last, weights, k_hbm, v_hbm, tail, sem):
    me = lax.axis_index("tp")
    mate = me + 1 - 2 * lax.rem(me, 2)
    steps, n_layers, block, both = res.shape
    head_dim = both // 2
    piece = block // PIECES
    copies = []

    def put(src, rows):
        for side, dst in enumerate((k_hbm, v_hbm)):
            copy = pltpu.make_async_copy(src.at[:, :, pl.ds(side * head_dim, head_dim)], dst.at[:, rows, :], sem.at[len(copies)])
            copy.start()
            copies.append(copy)

    def put_arrival(src, j):
        away = 2 + 2 * (j // PIECES)
        for group in range(4):
            who = me if group < 2 else mate
            if group % 2 == 0:
                start = lax.rem(who + n - away, n) * block + (j % PIECES) * piece
            else:
                start = lax.rem(who + away, n) * block + ((j + PIECES // 2) % PIECES) * piece
            put(src.at[:, pl.ds(group * piece, piece)], pl.ds(pl.multiple_of(start, piece), piece))

    put(res.at[0], pl.ds(pl.multiple_of(me * block, block), block))
    put(res.at[1], pl.ds(pl.multiple_of(mate * block, block), block))
    for step in range(2, steps):
        put_arrival(res.at[step], step - 2)
    for layer in range(n_layers):
        tail[layer] = jnp.dot(last[...], weights[layer], preferred_element_type=jnp.float32).astype(jnp.bfloat16)
    put_arrival(tail, steps - 2)
    for copy in copies:
        copy.wait()


def solution(mesh):
    n = mesh.shape["tp"]

    def per_device(enc_out, norm_scale, w_key, w_value):
        _, block, d_model = enc_out.shape
        n_layers, _, _, head_dim = w_key.shape
        arrivals = (n // 2 - 1) * PIECES // 2
        anywhere = pl.BlockSpec(memory_space=pl.ANY)
        in_vmem = pl.BlockSpec(memory_space=pltpu.VMEM)
        res, last, weights = pl.pallas_call(
            functools.partial(ring_body, n),
            out_shape=(
                pltpu.VMEM((arrivals + 1, n_layers, block, 2 * head_dim), jnp.bfloat16),
                pltpu.VMEM((block, d_model), jnp.bfloat16),
                pltpu.VMEM((n_layers, d_model, 2 * head_dim), jnp.bfloat16),
            ),
            in_specs=[anywhere, in_vmem, anywhere, anywhere],
            out_specs=(in_vmem, in_vmem, in_vmem),
            scratch_shapes=[
                pltpu.VMEM((block, d_model), jnp.bfloat16),
                pltpu.VMEM((arrivals + 1, block, d_model), jnp.bfloat16),
                pltpu.SemaphoreType.DMA((PIECES,)),
                pltpu.SemaphoreType.DMA((2 * n_layers,)),
                pltpu.SemaphoreType.DMA((arrivals,)),
                pltpu.SemaphoreType.DMA((arrivals,)),
                pltpu.SemaphoreType.DMA((arrivals,)),
                pltpu.SemaphoreType.DMA((arrivals,)),
                pltpu.SemaphoreType.DMA((arrivals + 1,)),
                pltpu.SemaphoreType.DMA((arrivals + 1,)),
            ],
            compiler_params=pltpu.CompilerParams(collective_id=0, has_side_effects=True, vmem_limit_bytes=22 * 1024 * 1024),
            name="ring_project",
        )(enc_out.reshape(block, d_model), norm_scale, w_key.reshape(n_layers, d_model, head_dim), w_value.reshape(n_layers, d_model, head_dim))
        side = jax.ShapeDtypeStruct((n_layers, n * block, head_dim), jnp.bfloat16)
        keys, values = pl.pallas_call(
            functools.partial(place_body, n),
            out_shape=(side, side),
            in_specs=[in_vmem, in_vmem, in_vmem],
            out_specs=(anywhere, anywhere),
            scratch_shapes=[
                pltpu.VMEM((n_layers, block, 2 * head_dim), jnp.bfloat16),
                pltpu.SemaphoreType.DMA((4 + 8 * arrivals,)),
            ],
            compiler_params=pltpu.CompilerParams(vmem_limit_bytes=4 * 1024 * 1024),
            name="place",
        )(res, last, weights)
        shape = (n_layers, 1, n * block, 1, head_dim)
        return keys.reshape(shape), values.reshape(shape)

    weight_spec = P(None, None, "tp", None)
    cache_spec = P(None, "dp", None, "tp", None)
    return jax.shard_map(per_device, mesh=mesh, in_specs=(P("dp", "tp", None), P(None), weight_spec, weight_spec), out_specs=(cache_spec, cache_spec), check_vma=False)
```

time: 180 us -> 100 us (0.56)
  Pallas kernels: 0 us -> 99 us
  waiting for transfers between devices: 97.2 us -> 0 us
  matrix products: 64 us -> 0 us
  between operations: 14.1 us -> 0.82 us
  other arithmetic: 4.75 us -> 0 us
    pallas_call x0 -> x2, Pallas kernels: none -> 99 us  [the longest x1 93.2 us: per_device(): pl.pallas_call(functools.partial(ring_body, n), out_shape=(pltpu.VMEM((ar...]
    all_gather x1 -> x0, waiting for transfers between devices: 97.2 us -> none  [per_device(): gathered = lax.all_gather(normed, 'tp', axis=1, tiled=True)]
    dot_general x2 -> x0, matrix products: 64 us -> none  [the longest x1 33.8 us: per_device(): jnp.einsum('bsd,ldhk->lbshk', gathered, w_value, preferred_element_type=j...]
    convert_element_type x2 -> x0, other arithmetic: 3.22 us -> none  [the longest x1 2.52 us: rms_norm(): (acts * lax.rsqrt(mean_sq + NORM_EPS) * norm_scale.astype(jnp.float32)).a...]
  transfers between devices with their start and end apart: 1 -> 0, of which waited for: 1 -> 0; matrix products, arithmetic and copies ran while one was open for 0% -> 0% of each run, Pallas kernels for 0% -> 0%
where the time goes in v2:
time: 100 us; the launch traced here: 99.8 us
  Pallas kernels  99 us (99%)
    pallas_call x1, Pallas kernels, per_device(): pl.pallas_call(functools.partial(ring_body, n), out_shape=(pltpu.VMEM((ar...  93.2 us
    pallas_call x1, Pallas kernels, per_device(): pl.pallas_call(functools.partial(place_body, n), out_shape=(side, side),...  5.82 us

profile of v2, /device:TPU:21, one launch (start us, length us, event | category | flops | bytes accessed | tf_op | source)
XLA Modules:
  0.0 99.8 jit_solution(5213053671356101488)
XLA Ops:
  0.6 93.2 %ring_project.1 = (bf16[15,6,128,512]{3,2,1,0:T(8,128)(2,1)S(1)}, bf16[128,4096]{1,0:T(8,128)(2,1)S(1)}, bf16[6,4096,512]{2,1,0:T(8,128)(2,1)S(1)}) custom-call(bf16[128,4096]{1,0:T(8,128)(2,1)} %bitcast.11, bf16[4096]{0:T(1024)(128)(2,1)} %scale_ref.1, bf16[6,4096,256]{2,1,0:T(8,128)(2,1)} %bitcast.9, bf16[6,4096,256]{2,1,0:T(8,128)(2,1)} %bitcast.10), custom_call_target="tpu_custom_call" | custom-call | tf_op jit(solution)/shard_map/ring_project/pallas_call | solution.py:192
  93.8 5.8 %place.1 = (bf16[6,2048,256]{2,1,0:T(8,128)(2,1)}, bf16[6,2048,256]{2,1,0:T(8,128)(2,1)}) custom-call(bf16[15,6,128,512]{3,2,1,0:T(8,128)(2,1)S(1)} %get-tuple-element.7.res, bf16[128,4096]{1,0:T(8,128)(2,1)S(1)} %get-tuple-element.8.last, bf16[6,4096,512]{2,1,0:T(8,128)(2,1)S(1)} %get-tuple-element.9.weights), custom_call_target="tpu_custom_call" | custom-call | tf_op jit(solution)/shard_map/place/pallas_call | solution.py:217

commit v3 on v2

--- a/solution.py
+++ b/solution.py
@@ -11,6 +11,24 @@
 MESH = pl.DeviceIdType.MESH
 NORM_ROWS = 16
 PIECES = 4
+CUTS = 4
+
+
+def token_starts(n, block, step):
+    me = lax.axis_index("tp")
+    mate = me + 1 - 2 * lax.rem(me, 2)
+    piece = block // PIECES
+    starts = []
+    for group in range(4):
+        if step < 2:
+            start = (mate if step else me) * block + group * piece
+        else:
+            away = 2 + 2 * ((step - 2) // PIECES)
+            who = me if group < 2 else mate
+            owner = lax.rem(who + away, n) if group % 2 else lax.rem(who + n - away, n)
+            start = owner * block + (step - 2 + group % 2 * PIECES // 2) % PIECES * piece
+        starts.append(pl.multiple_of(start, piece))
+    return starts
 
 
 def ring_body(n, x_hbm, scale_ref, wk_hbm, wv_hbm, out, last, weights, acts, tokens, in_sem, w_sem, cw_send, cw_recv, ccw_send, ccw_recv, mate_send, mate_recv):
@@ -59,30 +77,38 @@
         return last if j == arrivals - 1 else tokens.at[j + 2]
 
     def send_ring(j):
+        cuts = CUTS if j == arrivals - 1 else 1
         for side, (send_sem, recv_sem, other) in enumerate(((cw_send, cw_recv, after), (ccw_send, ccw_recv, before))):
             if j < PIECES:
                 own = (j + side * PIECES // 2) % PIECES
                 src = tokens.at[0, pl.ds(own * piece, piece)]
             else:
                 src = landing(j - PIECES).at[pl.ds(side * piece, piece)]
-            send((side, j), src, landing(j).at[pl.ds(side * piece, piece)], send_sem.at[j], recv_sem.at[j], other)
-
-    def handle(j):
-        waits[0, j].wait_recv()
-        waits[1, j].wait_recv()
+            dst = landing(j).at[pl.ds(side * piece, piece)]
+            for cut in range(cuts):
+                columns = pl.ds(cut * d_model // cuts, d_model // cuts)
+                send((side, j, cut), src.at[:, columns], dst.at[:, columns], send_sem.at[j + cut], recv_sem.at[j + cut], other)
+
+    def handle(j, cut=0):
+        waits[0, j, cut].wait_recv()
+        waits[1, j, cut].wait_recv()
         if j + PIECES < arrivals:
             send_ring(j + PIECES)
-        here = landing(j)
-        send((2, j), here.at[pl.ds(0, block // 2)], here.at[pl.ds(block // 2, block // 2)], mate_send.at[j + 1], mate_recv.at[j + 1], mate)
-
-    def swapped(j):
-        waits[2, j].wait_recv()
+        cuts = CUTS if j == arrivals - 1 else 1
+        here = landing(j).at[:, pl.ds(cut * d_model // cuts, d_model // cuts)]
+        send((2, j, cut), here.at[pl.ds(0, block // 2)], here.at[pl.ds(block // 2, block // 2)], mate_send.at[j + cut + 1], mate_recv.at[j + cut + 1], mate)
+
+    def swapped(j, cut=0):
+        waits[2, j, cut].wait_recv()
 
     def project(step, count, layer):
         rows = tokens[pl.ds(step, count)].reshape(count * block, d_model)
         both_sides = jnp.dot(rows, weights[layer], preferred_element_type=jnp.float32).astype(jnp.bfloat16)
         for i in range(count):
-            out[step + i, layer] = both_sides[i * block : (i + 1) * block]
+            for group, start in enumerate(token_starts(n, block, step + i)):
+                first = i * block + group * piece
+                for side in range(2):
+                    out[side, layer, pl.ds(start, piece)] = both_sides[first : first + piece, side * head_dim : (side + 1) * head_dim]
 
     x_copies[0].wait()
     x_copies[1].wait()
@@ -99,7 +125,7 @@
     normalize(3)
     for j in range(1, PIECES):
         send_ring(j)
-    send((2, -1), tokens.at[0], tokens.at[1], mate_send.at[0], mate_recv.at[0], mate)
+    send((2, -1, 0), tokens.at[0], tokens.at[1], mate_send.at[0], mate_recv.at[0], mate)
     swapped(-1)
 
     @pl.loop(0, n_layers)
@@ -108,74 +134,86 @@
             copy.wait()
         project(0, 2, layer)
 
-    late = arrivals - 6
-    for j in range(0, late, 2):
+    def project_pair(j, first, stop):
+        loops = (stop - first) // 2
+
+        @pl.loop(0, loops)
+        def _(i):
+            project(j + 2, 2, first + 2 * i)
+            project(j + 2, 2, first + 2 * i + 1)
+
+        for layer in range(first + 2 * loops, stop):
+            project(j + 2, 2, layer)
+
+    end = arrivals - 1
+    handle(0)
+    handle(1)
+    for j in range(2, end - 5, 2):
         handle(j)
+        swapped(j - 2)
+        swapped(j - 1)
+        project_pair(j - 2, 0, n_layers)
         handle(j + 1)
-        swapped(j)
-        swapped(j + 1)
-
-        @pl.loop(0, n_layers)
-        def _(layer):
-            project(j + 2, 2, layer)
-
-    handle(late)
-    handle(late + 1)
-    swapped(late)
-    swapped(late + 1)
-    for layer in range(n_layers):
-        project(late + 2, 2, layer)
-        if layer == n_layers // 2:
-            handle(late + 2)
-    swapped(late + 2)
-    for layer in range(n_layers):
-        project(late + 4, 1, layer)
-        if layer == n_layers - 2:
-            handle(late + 3)
-    swapped(late + 3)
-    for layer in range(n_layers):
-        project(late + 5, 1, layer)
-    handle(late + 4)
-    swapped(late + 4)
-    for layer in range(n_layers):
-        project(late + 6, 1, layer)
-    handle(late + 5)
-    swapped(late + 5)
+    handle(end - 5)
+    swapped(end - 7)
+    swapped(end - 6)
+    project_pair(end - 7, 0, n_layers - 1)
+    handle(end - 4)
+    project_pair(end - 7, n_layers - 1, n_layers)
+    swapped(end - 5)
+    swapped(end - 4)
+    project_pair(end - 5, 0, n_layers // 2)
+    handle(end - 3)
+    project_pair(end - 5, n_layers // 2, n_layers)
+    swapped(end - 3)
+    for layer in range(n_layers):
+        if layer == 2:
+            handle(end - 2)
+        project(end - 1, 1, layer)
+    swapped(end - 2)
+    for layer in range(n_layers):
+        project(end, 1, layer)
+    handle(end - 1)
+    swapped(end - 1)
+    after_layer = {1: (0, 1), 2: (2,), 3: (3,)}
+    for layer in range(n_layers):
+        project(end + 1, 1, layer)
+        for cut in after_layer.get(layer, ()):
+            handle(end, cut)
+    for cut in range(CUTS):
+        swapped(end, cut)
     for copy in sends:
         copy.wait_send()
 
 
 def place_body(n, res, last, weights, k_hbm, v_hbm, tail, sem):
     me = lax.axis_index("tp")
-    mate = me + 1 - 2 * lax.rem(me, 2)
-    steps, n_layers, block, both = res.shape
-    head_dim = both // 2
+    _, n_layers, _, head_dim = res.shape
+    block = last.shape[0]
     piece = block // PIECES
+    steps = (n // 2 - 1) * PIECES // 2 + 2
     copies = []
 
-    def put(src, rows):
-        for side, dst in enumerate((k_hbm, v_hbm)):
-            copy = pltpu.make_async_copy(src.at[:, :, pl.ds(side * head_dim, head_dim)], dst.at[:, rows, :], sem.at[len(copies)])
-            copy.start()
-            copies.append(copy)
-
-    def put_arrival(src, j):
-        away = 2 + 2 * (j // PIECES)
-        for group in range(4):
-            who = me if group < 2 else mate
-            if group % 2 == 0:
-                start = lax.rem(who + n - away, n) * block + (j % PIECES) * piece
-            else:
-                start = lax.rem(who + away, n) * block + ((j + PIECES // 2) % PIECES) * piece
-            put(src.at[:, pl.ds(group * piece, piece)], pl.ds(pl.multiple_of(start, piece), piece))
-
-    put(res.at[0], pl.ds(pl.multiple_of(me * block, block), block))
-    put(res.at[1], pl.ds(pl.multiple_of(mate * block, block), block))
-    for step in range(2, steps):
-        put_arrival(res.at[step], step - 2)
+    def put(src, side, rows, layers=slice(None)):
+        copy = pltpu.make_async_copy(src, (k_hbm, v_hbm)[side].at[layers, rows], sem.at[len(copies)])
+        copy.start()
+        copies.append(copy)
+
+    chip = me // 2
+    for away in range(n // 2):
+        if away != n // 4:
+            rows = pl.ds(pl.multiple_of(lax.rem(chip + away, n // 2) * 2 * block, 2 * block), 2 * block)
+            for side in range(2):
+                put(res.at[side, :, rows], side, rows)
+    for start in token_starts(n, block, steps - 2):
+        rows = pl.ds(start, piece)
+        for side in range(2):
+            put(res.at[side, :, rows], side, rows)
     for layer in range(n_layers):
         tail[layer] = jnp.dot(last[...], weights[layer], preferred_element_type=jnp.float32).astype(jnp.bfloat16)
-    put_arrival(tail, steps - 2)
+        for group, start in enumerate(token_starts(n, block, steps - 1)):
+            for side in range(2):
+                put(tail.at[pl.ds(layer, 1), pl.ds(group * piece, piece), pl.ds(side * head_dim, head_dim)], side, pl.ds(start, piece), pl.ds(layer, 1))
     for copy in copies:
         copy.wait()
 
@@ -192,7 +230,7 @@
         res, last, weights = pl.pallas_call(
             functools.partial(ring_body, n),
             out_shape=(
-                pltpu.VMEM((arrivals + 1, n_layers, block, 2 * head_dim), jnp.bfloat16),
+                pltpu.VMEM((2, n_layers, n * block, head_dim), jnp.bfloat16),
                 pltpu.VMEM((block, d_model), jnp.bfloat16),
                 pltpu.VMEM((n_layers, d_model, 2 * head_dim), jnp.bfloat16),
             ),
@@ -203,12 +241,12 @@
                 pltpu.VMEM((arrivals + 1, block, d_model), jnp.bfloat16),
                 pltpu.SemaphoreType.DMA((PIECES,)),
                 pltpu.SemaphoreType.DMA((2 * n_layers,)),
-                pltpu.SemaphoreType.DMA((arrivals,)),
-                pltpu.SemaphoreType.DMA((arrivals,)),
-                pltpu.SemaphoreType.DMA((arrivals,)),
-                pltpu.SemaphoreType.DMA((arrivals,)),
-                pltpu.SemaphoreType.DMA((arrivals + 1,)),
-                pltpu.SemaphoreType.DMA((arrivals + 1,)),
+                pltpu.SemaphoreType.DMA((arrivals + CUTS - 1,)),
+                pltpu.SemaphoreType.DMA((arrivals + CUTS - 1,)),
+                pltpu.SemaphoreType.DMA((arrivals + CUTS - 1,)),
+                pltpu.SemaphoreType.DMA((arrivals + CUTS - 1,)),
+                pltpu.SemaphoreType.DMA((arrivals + CUTS,)),
+                pltpu.SemaphoreType.DMA((arrivals + CUTS,)),
             ],
             compiler_params=pltpu.CompilerParams(collective_id=0, has_side_effects=True, vmem_limit_bytes=22 * 1024 * 1024),
             name="ring_project",
@@ -221,7 +259,7 @@
             out_specs=(anywhere, anywhere),
             scratch_shapes=[
                 pltpu.VMEM((n_layers, block, 2 * head_dim), jnp.bfloat16),
-                pltpu.SemaphoreType.DMA((4 + 8 * arrivals,)),
+                pltpu.SemaphoreType.DMA((n + 6 + 8 * n_layers,)),
             ],
             compiler_params=pltpu.CompilerParams(vmem_limit_bytes=4 * 1024 * 1024),
             name="place",

time: 100 us -> 98.8 us (0.988)
  Pallas kernels: 99 us -> 97.8 us
where the time goes in v3:
time: 98.8 us; the launch traced here: 98.6 us
  Pallas kernels  97.8 us (99%)
    pallas_call x1, Pallas kernels, per_device(): pl.pallas_call(functools.partial(ring_body, n), out_shape=(pltpu.VMEM((2,...  92.7 us
    pallas_call x1, Pallas kernels, per_device(): pl.pallas_call(functools.partial(place_body, n), out_shape=(side, side),...  5.16 us

profile of v3, /device:TPU:21, one launch (start us, length us, event | category | flops | bytes accessed | tf_op | source)
XLA Modules:
  0.0 98.6 jit_solution(12278163147139770073)
XLA Ops:
  0.6 92.7 %ring_project.1 = (bf16[2,6,2048,256]{3,2,1,0:T(8,128)(2,1)S(1)}, bf16[128,4096]{1,0:T(8,128)(2,1)S(1)}, bf16[6,4096,512]{2,1,0:T(8,128)(2,1)S(1)}) custom-call(bf16[128,4096]{1,0:T(8,128)(2,1)} %bitcast.11, bf16[4096]{0:T(1024)(128)(2,1)} %scale_ref.1, bf16[6,4096,256]{2,1,0:T(8,128)(2,1)} %bitcast.9, bf16[6,4096,256]{2,1,0:T(8,128)(2,1)} %bitcast.10), custom_call_target="tpu_custom_call" | custom-call | tf_op jit(solution)/shard_map/ring_project/pallas_call | solution.py:230
  93.3 5.2 %place.1 = (bf16[6,2048,256]{2,1,0:T(8,128)(2,1)}, bf16[6,2048,256]{2,1,0:T(8,128)(2,1)}) custom-call(bf16[2,6,2048,256]{3,2,1,0:T(8,128)(2,1)S(1)} %get-tuple-element.7.res, bf16[128,4096]{1,0:T(8,128)(2,1)S(1)} %get-tuple-element.8.last, bf16[6,4096,512]{2,1,0:T(8,128)(2,1)S(1)} %get-tuple-element.9.weights), custom_call_target="tpu_custom_call" | custom-call | tf_op jit(solution)/shard_map/place/pallas_call | solution.py:255

commit v4 on v3

--- a/solution.py
+++ b/solution.py
@@ -11,6 +11,7 @@
 MESH = pl.DeviceIdType.MESH
 NORM_ROWS = 16
 PIECES = 4
+OPENING = 2
 CUTS = 4
 
 
@@ -31,7 +32,7 @@
     return starts
 
 
-def ring_body(n, x_hbm, scale_ref, wk_hbm, wv_hbm, out, last, weights, acts, tokens, in_sem, w_sem, cw_send, cw_recv, ccw_send, ccw_recv, mate_send, mate_recv):
+def ring_body(n, x_hbm, scale_hbm, wk_hbm, wv_hbm, out, last, weights, acts, scale_ref, tokens, in_sem, w_sem, cw_send, cw_recv, ccw_send, ccw_recv, mate_send, mate_recv):
     me = lax.axis_index("tp")
     mate = me + 1 - 2 * lax.rem(me, 2)
     after = lax.rem(me + 2, n)
@@ -42,6 +43,8 @@
     head_dim = both // 2
     arrivals = (n // 2 - 1) * PIECES // 2
 
+    scale_copy = pltpu.make_async_copy(scale_hbm, scale_ref, in_sem.at[PIECES])
+    scale_copy.start()
     x_copies = []
     for part in (0, 2, 1, 3):
         rows = pl.ds(part * piece, piece)
@@ -50,19 +53,16 @@
     barrier = pltpu.get_barrier_semaphore()
     for other in (after, before, mate):
         pl.semaphore_signal(barrier, inc=1, device_id={"tp": other}, device_id_type=MESH)
-    scale = scale_ref[...].reshape(1, d_model).astype(jnp.float32)
-
     def load_weights(layer):
         for side, src in enumerate((wk_hbm, wv_hbm)):
             yield pltpu.make_async_copy(src.at[layer], weights.at[layer, :, pl.ds(side * head_dim, head_dim)], w_sem.at[2 * layer + side])
 
-    def normalize(part):
-        @pl.loop(0, piece // NORM_ROWS)
-        def _(i):
-            rows = pl.ds(pl.multiple_of(part * piece + i * NORM_ROWS, NORM_ROWS), NORM_ROWS)
-            x = acts[rows, :].astype(jnp.float32)
-            mean_sq = jnp.mean(x * x, axis=-1, keepdims=True)
-            tokens[0, rows, :] = (x * lax.rsqrt(mean_sq + NORM_EPS) * scale).astype(jnp.bfloat16)
+    def normalize(start):
+        rows = pl.ds(start, NORM_ROWS)
+        x = acts[rows, :].astype(jnp.float32)
+        scale = scale_ref[...].reshape(1, d_model).astype(jnp.float32)
+        mean_sq = jnp.mean(x * x, axis=-1, keepdims=True)
+        tokens[0, rows, :] = (x * lax.rsqrt(mean_sq + NORM_EPS) * scale).astype(jnp.bfloat16)
 
     sends = []
     waits = {}
@@ -87,11 +87,19 @@
             dst = landing(j).at[pl.ds(side * piece, piece)]
             for cut in range(cuts):
                 columns = pl.ds(cut * d_model // cuts, d_model // cuts)
-                send((side, j, cut), src.at[:, columns], dst.at[:, columns], send_sem.at[j + cut], recv_sem.at[j + cut], other)
+                at = j + cut + OPENING - 1
+                send((side, j, cut), src.at[:, columns], dst.at[:, columns], send_sem.at[at], recv_sem.at[at], other)
+
+    def send_opening(cut):
+        size = piece // OPENING
+        for side, (send_sem, recv_sem, other) in enumerate(((cw_send, cw_recv, after), (ccw_send, ccw_recv, before))):
+            src = tokens.at[0, pl.ds(side * (PIECES // 2) * piece + cut * size, size)]
+            send((side, 0, cut), src, landing(0).at[pl.ds(side * piece + cut * size, size)], send_sem.at[cut], recv_sem.at[cut], other)
 
     def handle(j, cut=0):
-        waits[0, j, cut].wait_recv()
-        waits[1, j, cut].wait_recv()
+        for part in range(OPENING) if j == 0 else (cut,):
+            waits[0, j, part].wait_recv()
+            waits[1, j, part].wait_recv()
         if j + PIECES < arrivals:
             send_ring(j + PIECES)
         cuts = CUTS if j == arrivals - 1 else 1
@@ -110,19 +118,24 @@
                 for side in range(2):
                     out[side, layer, pl.ds(start, piece)] = both_sides[first : first + piece, side * head_dim : (side + 1) * head_dim]
 
+    scale_copy.wait()
     x_copies[0].wait()
     x_copies[1].wait()
     for layer in range(n_layers):
         for copy in load_weights(layer):
             copy.start()
-    normalize(0)
-    normalize(2)
-    pl.semaphore_wait(barrier, 3)
-    send_ring(0)
+    for cut in range(OPENING):
+        for side in range(2):
+            for start in range(0, piece // OPENING, NORM_ROWS):
+                normalize((side * (PIECES // 2) * OPENING + cut) * (piece // OPENING) + start)
+        if cut == 0:
+            pl.semaphore_wait(barrier, 3)
+        send_opening(cut)
     x_copies[2].wait()
     x_copies[3].wait()
-    normalize(1)
-    normalize(3)
+    for part in (1, 3):
+        for start in range(0, piece, NORM_ROWS):
+            normalize(part * piece + start)
     for j in range(1, PIECES):
         send_ring(j)
     send((2, -1, 0), tokens.at[0], tokens.at[1], mate_send.at[0], mate_recv.at[0], mate)
@@ -234,17 +247,18 @@
                 pltpu.VMEM((block, d_model), jnp.bfloat16),
                 pltpu.VMEM((n_layers, d_model, 2 * head_dim), jnp.bfloat16),
             ),
-            in_specs=[anywhere, in_vmem, anywhere, anywhere],
+            in_specs=[anywhere, anywhere, anywhere, anywhere],
             out_specs=(in_vmem, in_vmem, in_vmem),
             scratch_shapes=[
                 pltpu.VMEM((block, d_model), jnp.bfloat16),
+                pltpu.VMEM((d_model,), jnp.bfloat16),
                 pltpu.VMEM((arrivals + 1, block, d_model), jnp.bfloat16),
-                pltpu.SemaphoreType.DMA((PIECES,)),
+                pltpu.SemaphoreType.DMA((PIECES + 1,)),
                 pltpu.SemaphoreType.DMA((2 * n_layers,)),
-                pltpu.SemaphoreType.DMA((arrivals + CUTS - 1,)),
-                pltpu.SemaphoreType.DMA((arrivals + CUTS - 1,)),
-                pltpu.SemaphoreType.DMA((arrivals + CUTS - 1,)),
-                pltpu.SemaphoreType.DMA((arrivals + CUTS - 1,)),
+                pltpu.SemaphoreType.DMA((arrivals + CUTS + OPENING - 2,)),
+                pltpu.SemaphoreType.DMA((arrivals + CUTS + OPENING - 2,)),
+                pltpu.SemaphoreType.DMA((arrivals + CUTS + OPENING - 2,)),
+                pltpu.SemaphoreType.DMA((arrivals + CUTS + OPENING - 2,)),
                 pltpu.SemaphoreType.DMA((arrivals + CUTS,)),
                 pltpu.SemaphoreType.DMA((arrivals + CUTS,)),
             ],

time: 98.8 us -> 97.7 us (0.989)
  Pallas kernels: 97.8 us -> 96.8 us
    pallas_call x1, Pallas kernels: 92.7 us -> 91.6 us  [per_device(): pl.pallas_call(functools.partial(ring_body, n), out_shape=(pltpu.VMEM((2,...]
where the time goes in v4:
time: 97.7 us; the launch traced here: 97.6 us
  Pallas kernels  96.8 us (99%)
    pallas_call x1, Pallas kernels, per_device(): pl.pallas_call(functools.partial(ring_body, n), out_shape=(pltpu.VMEM((2,...  91.6 us
    pallas_call x1, Pallas kernels, per_device(): pl.pallas_call(functools.partial(place_body, n), out_shape=(side, side),...  5.16 us

profile of v4, /device:TPU:21, one launch (start us, length us, event | category | flops | bytes accessed | tf_op | source)
XLA Modules:
  0.0 97.6 jit_solution(1913585176085434914)
XLA Ops:
  0.6 91.6 %ring_project.1 = (bf16[2,6,2048,256]{3,2,1,0:T(8,128)(2,1)S(1)}, bf16[128,4096]{1,0:T(8,128)(2,1)S(1)}, bf16[6,4096,512]{2,1,0:T(8,128)(2,1)S(1)}) custom-call(bf16[128,4096]{1,0:T(8,128)(2,1)} %bitcast.11, bf16[4096]{0:T(1024)(128)(2,1)} %scale_hbm.1, bf16[6,4096,256]{2,1,0:T(8,128)(2,1)} %bitcast.9, bf16[6,4096,256]{2,1,0:T(8,128)(2,1)} %bitcast.10), custom_call_target="tpu_custom_call" | custom-call | tf_op jit(solution)/shard_map/ring_project/pallas_call | solution.py:243
  92.2 5.2 %place.1 = (bf16[6,2048,256]{2,1,0:T(8,128)(2,1)}, bf16[6,2048,256]{2,1,0:T(8,128)(2,1)}) custom-call(bf16[2,6,2048,256]{3,2,1,0:T(8,128)(2,1)S(1)} %get-tuple-element.7.res, bf16[128,4096]{1,0:T(8,128)(2,1)S(1)} %get-tuple-element.8.last, bf16[6,4096,512]{2,1,0:T(8,128)(2,1)S(1)} %get-tuple-element.9.weights), custom_call_target="tpu_custom_call" | custom-call | tf_op jit(solution)/shard_map/place/pallas_call | solution.py:269

commit v5 on v4

--- a/solution.py
+++ b/solution.py
@@ -85,7 +85,7 @@
             else:
                 src = landing(j - PIECES).at[pl.ds(side * piece, piece)]
             dst = landing(j).at[pl.ds(side * piece, piece)]
-            for cut in range(cuts):
+            for cut in range(max(cuts - 1, 1)):
                 columns = pl.ds(cut * d_model // cuts, d_model // cuts)
                 at = j + cut + OPENING - 1
                 send((side, j, cut), src.at[:, columns], dst.at[:, columns], send_sem.at[at], recv_sem.at[at], other)
@@ -95,6 +95,50 @@
         for side, (send_sem, recv_sem, other) in enumerate(((cw_send, cw_recv, after), (ccw_send, ccw_recv, before))):
             src = tokens.at[0, pl.ds(side * (PIECES // 2) * piece + cut * size, size)]
             send((side, 0, cut), src, landing(0).at[pl.ds(side * piece + cut * size, size)], send_sem.at[cut], recv_sem.at[cut], other)
+
+    final = d_model // CUTS
+    whole = pl.ds(d_model - final, final)
+    kept = pl.ds(d_model - final, final // 2)
+    lent = pl.ds(d_model - final // 2, final // 2)
+    odd = lax.rem(me, 2) == 1
+    even = lax.rem(me, 2) == 0
+
+    def final_ring(lender, extra):
+        copies = []
+        for side, (send_sem, recv_sem, other) in enumerate(((cw_send, cw_recv, after), (ccw_send, ccw_recv, before))):
+            rows = pl.ds(side * piece + (block // 2 if extra else 0), piece)
+            columns = lent if extra else whole if lender else kept
+            at = arrivals + CUTS + OPENING - 3 + extra
+            copies.append(pltpu.make_async_remote_copy(src_ref=landing(arrivals - 1 - PIECES).at[rows, columns], dst_ref=last.at[rows, columns], send_sem=send_sem.at[at], recv_sem=recv_sem.at[at], device_id={"tp": other}, device_id_type=MESH))
+        return copies
+
+    def final_swap(lender):
+        mine, other = pl.ds(0, block // 2), pl.ds(block // 2, block // 2)
+        moves = [(mine, other, whole if lender else kept)] + ([(other, mine, lent)] if lender else [])
+        at = arrivals + CUTS - 1
+        return [pltpu.make_async_remote_copy(src_ref=last.at[src, columns], dst_ref=last.at[dst, columns], send_sem=mate_send.at[at + i], recv_sem=mate_recv.at[at + i], device_id={"tp": mate}, device_id_type=MESH) for i, (src, dst, columns) in enumerate(moves)]
+
+    def each_core(act):
+        pl.when(odd)(lambda: act(True))
+        pl.when(even)(lambda: act(False))
+
+    def final_send(lender):
+        for copy in final_ring(lender, 0) + (final_ring(lender, 1) if lender else []):
+            copy.start()
+
+    def final_handle(lender):
+        for copy in final_ring(lender, 0) + (final_ring(lender, 1) if lender else []):
+            copy.wait_recv()
+        for copy in final_swap(lender):
+            copy.start()
+
+    def final_swapped(lender):
+        for copy in final_swap(not lender):
+            copy.wait_recv()
+
+    def final_sent(lender):
+        for copy in final_ring(lender, 0) + (final_ring(lender, 1) if lender else []) + final_swap(lender):
+            copy.wait_send()
 
     def handle(j, cut=0):
         for part in range(OPENING) if j == 0 else (cut,):
@@ -175,6 +219,7 @@
     project_pair(end - 7, n_layers - 1, n_layers)
     swapped(end - 5)
     swapped(end - 4)
+    each_core(final_send)
     project_pair(end - 5, 0, n_layers // 2)
     handle(end - 3)
     project_pair(end - 5, n_layers // 2, n_layers)
@@ -192,9 +237,14 @@
     for layer in range(n_layers):
         project(end + 1, 1, layer)
         for cut in after_layer.get(layer, ()):
-            handle(end, cut)
-    for cut in range(CUTS):
+            if cut < CUTS - 1:
+                handle(end, cut)
+            else:
+                each_core(final_handle)
+    for cut in range(CUTS - 1):
         swapped(end, cut)
+    each_core(final_swapped)
+    each_core(final_sent)
     for copy in sends:
         copy.wait_send()
 
@@ -255,12 +305,12 @@
                 pltpu.VMEM((arrivals + 1, block, d_model), jnp.bfloat16),
                 pltpu.SemaphoreType.DMA((PIECES + 1,)),
                 pltpu.SemaphoreType.DMA((2 * n_layers,)),
-                pltpu.SemaphoreType.DMA((arrivals + CUTS + OPENING - 2,)),
-                pltpu.SemaphoreType.DMA((arrivals + CUTS + OPENING - 2,)),
-                pltpu.SemaphoreType.DMA((arrivals + CUTS + OPENING - 2,)),
-                pltpu.SemaphoreType.DMA((arrivals + CUTS + OPENING - 2,)),
-                pltpu.SemaphoreType.DMA((arrivals + CUTS,)),
-                pltpu.SemaphoreType.DMA((arrivals + CUTS,)),
+                pltpu.SemaphoreType.DMA((arrivals + CUTS + OPENING - 1,)),
+                pltpu.SemaphoreType.DMA((arrivals + CUTS + OPENING - 1,)),
+                pltpu.SemaphoreType.DMA((arrivals + CUTS + OPENING - 1,)),
+                pltpu.SemaphoreType.DMA((arrivals + CUTS + OPENING - 1,)),
+                pltpu.SemaphoreType.DMA((arrivals + CUTS + 1,)),
+                pltpu.SemaphoreType.DMA((arrivals + CUTS + 1,)),
             ],
             compiler_params=pltpu.CompilerParams(collective_id=0, has_side_effects=True, vmem_limit_bytes=22 * 1024 * 1024),
             name="ring_project",

time: 97.7 us -> 97.9 us (level)
  no operation moved by 1% of the time
where the time goes in v5:
time: 97.9 us; the launch traced here: 97.7 us
  Pallas kernels  96.9 us (99%)
    pallas_call x1, Pallas kernels, per_device(): pl.pallas_call(functools.partial(ring_body, n), out_shape=(pltpu.VMEM((2,...  91.8 us
    pallas_call x1, Pallas kernels, per_device(): pl.pallas_call(functools.partial(place_body, n), out_shape=(side, side),...  5.16 us

profile of v5, /device:TPU:21, one launch (start us, length us, event | category | flops | bytes accessed | tf_op | source)
XLA Modules:
  0.0 97.7 jit_solution(8123924479392842365)
XLA Ops:
  0.6 91.8 %ring_project.1 = (bf16[2,6,2048,256]{3,2,1,0:T(8,128)(2,1)S(1)}, bf16[128,4096]{1,0:T(8,128)(2,1)S(1)}, bf16[6,4096,512]{2,1,0:T(8,128)(2,1)S(1)}) custom-call(bf16[128,4096]{1,0:T(8,128)(2,1)} %bitcast.11, bf16[4096]{0:T(1024)(128)(2,1)} %scale_hbm.1, bf16[6,4096,256]{2,1,0:T(8,128)(2,1)} %bitcast.9, bf16[6,4096,256]{2,1,0:T(8,128)(2,1)} %bitcast.10), custom_call_target="tpu_custom_call" | custom-call | tf_op jit(solution)/shard_map/ring_project/pallas_call | solution.py:293
  92.4 5.2 %place.1 = (bf16[6,2048,256]{2,1,0:T(8,128)(2,1)}, bf16[6,2048,256]{2,1,0:T(8,128)(2,1)}) custom-call(bf16[2,6,2048,256]{3,2,1,0:T(8,128)(2,1)S(1)} %get-tuple-element.7.res, bf16[128,4096]{1,0:T(8,128)(2,1)S(1)} %get-tuple-element.8.last, bf16[6,4096,512]{2,1,0:T(8,128)(2,1)S(1)} %get-tuple-element.9.weights), custom_call_target="tpu_custom_call" | custom-call | tf_op jit(solution)/shard_map/place/pallas_call | solution.py:319
